TPU v7x, 256 devices: a whole 4x4x8 slice. The times are simulated.
256 devices in a mesh: img: 16 (over y, x), row: 16 (over z, core).
Axes of the slice: x: 4, y: 4, z: 8, core: 2. Of those that a mesh axis runs over, the one named last changes fastest.
Arguments:
- latent: bfloat16 [1024, 128, 512], P(('img', 'row')), parts along dimension 0, may hold values from -8 to 8
- attn_gain: float32 [512], replicated, may hold values from 0.5 to 1.5
- attn_shift: float32 [512], replicated, may hold values from -3 to 3
- w_query: bfloat16 [512, 512], replicated, may hold values from -2 to 2
- w_key: bfloat16 [512, 512], replicated, may hold values from -2 to 2
- w_value: bfloat16 [512, 512], replicated, may hold values from -0.25 to 0.25
- w_out: bfloat16 [512, 512], replicated, may hold values from -0.25 to 0.25
- conv_gain: float32 [512], replicated, may hold values from 0.5 to 1.5
- conv_shift: float32 [512], replicated, may hold values from -3 to 3
- w_conv: bfloat16 [3, 3, 512, 512], replicated, may hold values from -0.09375 to 0.09375
- conv_bias: float32 [512], replicated, may hold values from -3 to 3
Outputs:
- encoded: bfloat16 [1024, 128, 512], P(('img', 'row')), parts along dimension 0
There are 16 independent parts, one for each index of `img`. A program takes and returns all parts, laid end to end along the dimension named above; an argument that names none is the same for every part. Nothing has to cross between parts.
All inputs are finite; a program needn't handle non-finite values.
Results may differ from a plain program's by a relative error of at most 0.011.
Values may be sent and summed in bfloat16 or wider, within the bound.
No kernel may reach another device: no remote copies, remote signals or barrier semaphores. Data moves between devices by JAX's collectives and lax.ppermute only.
A program may use at most 128 MiB of HBM per device.

v0:
```python
import jax
import jax.numpy as jnp
from jax import lax
from jax.sharding import PartitionSpec as P

C = 512
GROUPS = 32
W = 128
epsilon = 1e-06


def copy_for_each(shard, axis):
    copies = jnp.broadcast_to(shard, (lax.axis_size(axis), *shard.shape))
    return lax.all_to_all(copies, axis, split_axis=0, concat_axis=0, tiled=True)


def taken_together(shard, axis):
    return copy_for_each(shard, axis).sum(axis=0)


def together(arrays, axis):
    line, at, done = (jnp.concatenate([a.reshape(-1) for a in arrays]), 0, [])
    total = taken_together(line, axis)
    for a in arrays:
        done.append(total[at : at + a.size].reshape(a.shape))
        at += a.size
    return tuple(done)


def with_halo(cells, sides, width):
    for axis, dim in sides:
        count = lax.axis_size(axis)
        ends = count - 1
        head = lax.slice_in_dim(cells, 0, width, axis=dim)
        tail = lax.slice_in_dim(cells, cells.shape[dim] - width, cells.shape[dim], axis=dim)
        cells = jnp.concatenate(
            [
                lax.ppermute(tail, axis, [(i, (i + 1) % count) for i in range(ends)]),
                cells,
                lax.ppermute(head, axis, [((i + 1) % count, i) for i in range(ends)]),
            ],
            axis=dim,
        )
    return cells


def group_stats(grouped, count):
    first, second = together(
        (jnp.sum(grouped, axis=(0, 2)), jnp.sum(grouped * grouped, axis=(0, 2))), "row"
    )
    centre = first / count
    spread = second / count - centre * centre
    return (centre, spread)


def group_norm(field, gain, shift):
    grouped = field.reshape(field.shape[0], GROUPS, C // GROUPS)
    count = field.shape[0] * lax.axis_size("row") * (C // GROUPS)
    centre, spread = group_stats(grouped, count)
    normed = (grouped - centre[None, :, None]) * lax.rsqrt(spread + epsilon)[None, :, None]
    return normed.reshape(field.shape) * gain + shift


def attend(carry, key_piece, value_piece, queries):
    maxima, denominator, accumulated = carry
    scaling = 1.0 / jnp.sqrt(jnp.float32(C))
    scores = (
        jnp.einsum("qc,kc->qk", queries, key_piece, preferred_element_type=jnp.float32) * scaling
    )
    newest = jnp.maximum(maxima, jnp.max(scores, axis=1))
    expo = jnp.exp(scores - newest[:, None])
    denominator = jnp.sum(expo, axis=1)
    accumulated = jnp.dot(
        expo.astype(jnp.bfloat16), value_piece, preferred_element_type=jnp.float32
    )
    return (newest, denominator, accumulated)


def local(
    latent,
    attn_gain,
    attn_shift,
    w_query,
    w_key,
    w_value,
    w_out,
    conv_gain,
    conv_shift,
    w_conv,
    conv_bias,
):
    local_rows = latent.shape[0]
    positions = latent.reshape(local_rows * W, C)
    normed = group_norm(positions.astype(jnp.float32), attn_gain, attn_shift).astype(jnp.bfloat16)
    queries = jnp.dot(normed, w_query, preferred_element_type=jnp.float32).astype(jnp.bfloat16)
    count_rows = positions.shape[0]
    start_carry = (
        jnp.full((count_rows,), -1e30, jnp.float32),
        jnp.zeros((count_rows,), jnp.float32),
        jnp.zeros((count_rows, C), jnp.float32),
    )
    piece = lax.all_gather(normed, "row", axis=0, tiled=True)
    key_piece = jnp.dot(piece, w_key, preferred_element_type=jnp.float32).astype(jnp.bfloat16)
    value_piece = jnp.dot(piece, w_value, preferred_element_type=jnp.float32).astype(jnp.bfloat16)
    maxima, denominator, accumulated = attend(start_carry, key_piece, value_piece, queries)
    attended = (accumulated / denominator[:, None]).astype(jnp.bfloat16)
    hidden = (
        positions.astype(jnp.float32) + jnp.dot(attended, w_out, preferred_element_type=jnp.float32)
    ).astype(jnp.bfloat16)
    activated = jax.nn.silu(group_norm(hidden.astype(jnp.float32), conv_gain, conv_shift)).astype(
        jnp.bfloat16
    )
    activated = activated.reshape(local_rows, W, C)
    bordered = with_halo(activated, (("row", 0),), 1)
    padded = jnp.pad(bordered, ((0, 0), (1, 1), (0, 0)))
    convolved = jnp.zeros((local_rows * W, C), jnp.float32)
    for row_tap in range(3):
        for col_tap in range(3):
            window = padded[row_tap : row_tap + local_rows, col_tap : col_tap + W].reshape(
                local_rows * W, C
            )
            convolved = convolved + jnp.dot(
                window, w_conv[row_tap, col_tap], preferred_element_type=jnp.float32
            )
    encoded = hidden.astype(jnp.float32) + (convolved + conv_bias)
    return encoded.astype(jnp.bfloat16).reshape(local_rows, W, C)


def solution(mesh):
    in_specs = (P(("img", "row"), None, None), P(), P(), P(), P(), P(), P(), P(), P(), P(), P())
    out_specs = P(("img", "row"), None, None)
    return jax.shard_map(local, mesh=mesh, in_specs=in_specs, out_specs=out_specs, check_vma=False)
```

profile of v0, /device:TPU:1, one launch (start us, length us, event | category | flops | bytes accessed | tf_op | source)
XLA Modules:
  0.0 157.1 jit_solution(7887998248014053439)
XLA Ops:
  6.5 0.0 copy-start
  6.5 0.0 all-gather.2.cloned.1.call-start
  6.5 1.3 convert_reduce_fusion.1
  7.8 0.1 reduce_sum.74
  7.9 0.1 reduce_sum.80
  8.0 0.1 reduce_sum.75
  8.1 0.1 reduce_sum.96
  8.2 0.1 pad_maximum_fusion.2
  8.3 16.8 %all_to_all.12 = f32[16,1,64]{2,1,0:T(1,128)S(1)} all-to-all(f32[16,1,64]{2,1,0:T(1,128)S(1)} %broadcast_in_dim.6), channel_id=1, replica_groups=mesh['img'=16,'row'=16] {'row'}, dimensions={0} | all-to-all | bytes 8192 | tf_op jit(solution)/shard_map/all_to_all | solution.py:14
  25.1 0.1 slice_multiply_fusion.1
  25.2 0.1 sub.40
  25.3 0.1 sub.41
  25.4 0.1 mul.68
  25.4 0.1 mul.69
  25.5 2.1 %fusion.31 = bf16[512,512]{1,0:T(8,128)(2,1)} fusion(bf16[4,128,512]{2,1,0:T(8,128)(2,1)} %param.11, f32[512]{0:T(512)} %param.13, f32[512]{0:T(512)} %param.12, f32[512]{0:T(512)S(1)} %mul.69, f32[512]{0:T(512)S(1)} %sub.41), kind=kLoop, calls=%fused_computation.46 | loop fusion | flops 1572864 | bytes 1056768 | tf_op jit(solution)/shard_map/convert_element_type | solution.py:94
  27.6 0.0 all-gather.2.cloned.1.call-update
  27.6 1.6 %convolution_convert_fusion.2 = bf16[512,512]{1,0:T(8,128)(2,1)S(1)} fusion(bf16[512,512]{1,0:T(8,128)(2,1)} %fusion.31, bf16[512,512]{1,0:T(8,128)(2,1)} %param.14), kind=kOutput, calls=%fused_computation.28 | convolution fusion | flops 268697600 | bytes 1572864 | tf_op jit(solution)/shard_map/dot_general | solution.py:95
  29.2 51.1 %all-gather.2.cloned.1.call-done = bf16[8192,512]{1,0:T(8,128)(2,1)} async-done(((bf16[512,512]{1,0:T(8,128)(2,1)}), bf16[8192,512]{1,0:T(8,128)(2,1)}) %all-gather.2.cloned.1.call-update) | async-done | bytes 8388624 | tf_op jit(solution)/shard_map/all_gather | solution.py:102
  80.4 0.0 copy-done
  80.4 14.5 %multiply_reduce_fusion = (f32[512]{0:T(512)S(1)}, f32[512,8192]{1,0:T(8,128)}) fusion(bf16[512,512]{1,0:T(8,128)(2,1)S(1)} %convolution_convert_fusion.2, bf16[8192,512]{1,0:T(8,128)(2,1)} %all-gather.2.cloned.1.call-done, bf16[512,512]{1,0:T(8,128)(2,1)S(1)} %copy-done), kind=kOutput, calls=%fused_computation.1 | convolution fusion | flops 8602517504 | bytes 26216448 | tf_op jit(solution)/shard_map/qc,kc->qk/dot_general | solution.py:68
  94.9 8.7 %fusion = f32[512]{0:T(512)S(1)} fusion(f32[512,8192]{1,0:T(8,128)} %get-tuple-element.24, f32[512]{0:T(512)S(1)} %broadcast_maximum_fusion), kind=kLoop, calls=%fused_computation.2 | loop fusion | flops 12582400 | bytes 16781312 | tf_op jit(solution)/shard_map/reduce_sum | solution.py:72
  103.6 0.0 copy-done.5
  103.6 0.0 copy-start.1
  103.6 0.0 copy-start.6
  103.6 0.0 copy-start.2
  103.6 0.0 copy-start.3
  103.6 17.2 %fusion.15 = bf16[512,512]{1,0:T(8,128)(2,1)S(1)} fusion(bf16[8192,512]{1,0:T(8,128)(2,1)} %all-gather.2.cloned.1.call-done, bf16[512,512]{1,0:T(8,128)(2,1)S(1)} %copy-done.5, f32[512,8192]{1,0:T(8,128)} %get-tuple-element.24, f32[512]{0:T(512)S(1)} %broadcast_maximum_fusion, f32[512]{0:T(512)S(1)} %fusion), kind=kOutput, calls=%fused_computation.31 | convolution fusion | flops 8607236096 | bytes 26218496 | tf_op jit(solution)/shard_map/dot_general | solution.py:73
  120.8 0.0 slice-start
  120.8 0.0 copy-done.1
  120.8 0.5 convert_reduce_fusion
  121.3 0.1 reduce_sum.100
  121.4 0.3 reduce_sum.101
  121.7 0.1 reduce_sum.103
  121.8 0.1 reduce_sum.104
  121.9 0.1 pad_maximum_fusion.3
  122.0 11.4 %all_to_all.13 = f32[16,1,64]{2,1,0:T(1,128)S(1)} all-to-all(f32[16,1,64]{2,1,0:T(1,128)S(1)} %broadcast_in_dim.8), channel_id=1, replica_groups=mesh['img'=16,'row'=16] {'row'}, dimensions={0} | all-to-all | bytes 8192 | tf_op jit(solution)/shard_map/all_to_all | solution.py:14
  133.4 0.1 slice_multiply_fusion
  133.5 0.1 sub.47
  133.6 0.1 sub.48
  133.7 0.1 mul.78
  133.7 0.1 mul.79
  133.8 0.0 copy-done.3
  133.8 0.4 fusion.27
  134.2 2.7 %collective-permute-start = (bf16[1,128,512]{2,1,0:T(8,128)(2,1)S(1)}, bf16[1,128,512]{2,1,0:T(8,128)(2,1)S(1)}, u32[]{:S(2)}, u32[]{:S(2)}) collective-permute-start(bf16[1,128,512]{2,1,0:T(8,128)(2,1)S(1)} %get-tuple-element.17), channel_id=1, source_target_pairs={{0,1},{1,2},{2,3},{3,4},{4,5},{5,6},{6,7},{7,8},{8,9},{9,10},{10,1... | collective-permute-start | bytes 393224 | tf_op jit(solution)/shard_map/ppermute | solution.py:38
  137.0 1.9 %collective-permute-start.1 = (bf16[1,128,512]{2,1,0:T(8,128)(2,1)S(1)}, bf16[1,128,512]{2,1,0:T(8,128)(2,1)S(1)}, u32[]{:S(2)}, u32[]{:S(2)}) collective-permute-start(bf16[1,128,512]{2,1,0:T(8,128)(2,1)S(1)} %get-tuple-element.18), channel_id=1, source_target_pairs={{1,0},{2,1},{3,2},{4,3},{5,4},{6,5},{7,6},{8,7},{9,8},{10,9},{11,1... | collective-permute-start | bytes 393224 | tf_op jit(solution)/shard_map/ppermute | solution.py:40
  138.9 0.0 collective-permute-done
  138.9 4.3 %collective-permute-done.1 = bf16[1,128,512]{2,1,0:T(8,128)(2,1)S(1)} collective-permute-done((bf16[1,128,512]{2,1,0:T(8,128)(2,1)S(1)}, bf16[1,128,512]{2,1,0:T(8,128)(2,1)S(1)}, u32[]{:S(2)}, u32[]{:S(2)}) %collective-permute-start.1) | collective-permute-done | bytes 131104 | tf_op jit(solution)/shard_map/ppermute | solution.py:40
  143.3 0.2 fusion.36
  143.5 0.0 slice-start.1
  143.5 0.4 fusion.58
  143.9 1.7 %fusion.46 = f32[512,512]{1,0:T(8,128)S(1)} fusion(bf16[512,512]{1,0:T(8,128)(2,1)S(1)} %bitcast.82, bf16[3,3,512,512]{3,2,1,0:T(8,128)(2,1)} %param.20), kind=kOutput, calls=%fused_computation.65 | convolution fusion | flops 268435456 | bytes 2097152 | tf_op jit(solution)/shard_map/dot_general | solution.py:122
  145.6 0.1 pad_maximum_fusion
  145.7 0.0 slice-done
  145.7 0.1 slice-done.1
  145.8 0.4 convolution_add_fusion.6
  146.3 0.0 copy-start.4
  146.3 0.4 convolution_add_fusion.5
  146.7 0.4 convolution_add_fusion.4
  147.2 0.4 convolution_add_fusion.3
  147.6 0.4 fusion.37
  148.1 0.4 convolution_add_fusion.2
  148.5 0.4 convolution_add_fusion.1
  149.0 0.0 copy-done.4
  149.0 1.3 fusion.10
  (10 shorter events, 0.1 us)
Async XLA Ops:
  6.5 73.8 %copy-start = (bf16[512,512]{1,0:T(8,128)(2,1)S(1)}, bf16[512,512]{1,0:T(8,128)(2,1)}, u32[]{:S(2)}) copy-start(bf16[512,512]{1,0:T(8,128)(2,1)} %param.15) | copy-start | bytes 1572868
  6.5 73.8 %all-gather.2.cloned.1.call-start = ((), (), s32[]{:S(2)}) async-start(), calls=%async_computation.2 | async-start | bytes 8912896 | tf_op jit(solution)/shard_map/all_gather | solution.py:102
  94.9 8.7 %copy-start.5 = (bf16[512,512]{1,0:T(8,128)(2,1)S(1)}, bf16[512,512]{1,0:T(8,128)(2,1)}, u32[]{:S(2)}) copy-start(bf16[512,512]{1,0:T(8,128)(2,1)} %param.16) | copy-start | bytes 1572868
  103.6 17.2 %copy-start.1 = (bf16[4,128,512]{2,1,0:T(8,128)(2,1)S(1)}, bf16[4,128,512]{2,1,0:T(8,128)(2,1)}, u32[]{:S(2)}) copy-start(bf16[4,128,512]{2,1,0:T(8,128)(2,1)} %param.11) | copy-start | bytes 1572868
  103.6 17.2 %copy-start.6 = (bf16[512,512]{1,0:T(8,128)(2,1)S(1)}, bf16[512,512]{1,0:T(8,128)(2,1)}, u32[]{:S(2)}) copy-start(bf16[512,512]{1,0:T(8,128)(2,1)} %param.17) | copy-start | bytes 1572868
  103.6 30.2 %copy-start.2 = (f32[512]{0:T(512)S(1)}, f32[512]{0:T(512)}, u32[]{:S(2)}) copy-start(f32[512]{0:T(512)} %param.19) | copy-start | bytes 6148
  103.6 30.2 %copy-start.3 = (f32[512]{0:T(512)S(1)}, f32[512]{0:T(512)}, u32[]{:S(2)}) copy-start(f32[512]{0:T(512)} %param.18) | copy-start | bytes 6148
  120.8 24.9 %slice-start = ((s8[4718592]{0:T(1024)(128)(4,1)}), s8[524288]{0:T(1024)(128)(4,1)S(1)}, s32[]{:S(2)}) async-start(s8[4718592]{0:T(1024)(128)(4,1)} %bitcast.74), calls=%async_computation.3 | async-start | bytes 1048576
  134.2 4.7 %collective-permute-start = (bf16[1,128,512]{2,1,0:T(8,128)(2,1)S(1)}, bf16[1,128,512]{2,1,0:T(8,128)(2,1)S(1)}, u32[]{:S(2)}, u32[]{:S(2)}) collective-permute-start(bf16[1,128,512]{2,1,0:T(8,128)(2,1)S(1)} %get-tuple-element.17), channel_id=1, source_target_pairs={{0,1},{1,2},{2,3},{3,4},{4,5},{5,6},{6,7},{7,8},{8,9},{9,10},{10,1... | collective-permute-start | bytes 393224 | tf_op jit(solution)/shard_map/ppermute | solution.py:38
  137.0 6.3 %collective-permute-start.1 = (bf16[1,128,512]{2,1,0:T(8,128)(2,1)S(1)}, bf16[1,128,512]{2,1,0:T(8,128)(2,1)S(1)}, u32[]{:S(2)}, u32[]{:S(2)}) collective-permute-start(bf16[1,128,512]{2,1,0:T(8,128)(2,1)S(1)} %get-tuple-element.18), channel_id=1, source_target_pairs={{1,0},{2,1},{3,2},{4,3},{5,4},{6,5},{7,6},{8,7},{9,8},{10,9},{11,1... | collective-permute-start | bytes 393224 | tf_op jit(solution)/shard_map/ppermute | solution.py:40
  143.5 2.3 %slice-start.1 = ((s8[4718592]{0:T(1024)(128)(4,1)}), s8[4194304]{0:T(1024)(128)(4,1)S(1)}, s32[]{:S(2)}) async-start(s8[4718592]{0:T(1024)(128)(4,1)} %bitcast.74), calls=%async_computation.4 | async-start | bytes 8388608
  146.3 2.7 %copy-start.4 = (f32[512]{0:T(512)S(1)}, f32[512]{0:T(512)}, u32[]{:S(2)}) copy-start(f32[512]{0:T(512)} %param.21) | copy-start | bytes 6148
Sparse Core Ops, SparseCore 0:
  27.7 52.6 all-gather.1
where the time goes:
time: 157 us
  waiting for transfers between devices  55.5 us (35%)
  matrix products  39.9 us (25%)
  blocking collectives  28.2 us (18%)
  other arithmetic  13.7 us (9%)
  between operations  13.6 us (9%)
  starting transfers between devices  4.64 us (3%)
    all_gather x1, waiting for transfers between devices, local(): piece = lax.all_gather(normed, 'row', axis=0, tiled=True)  51.1 us
    all_to_all x2, blocking collectives, copy_for_each(): return lax.all_to_all(copies, axis, split_axis=0, concat_axis=0, tiled=True)  28.2 us
    dot_general x1, matrix products, attend(): jnp.dot(expo.astype(jnp.bfloat16), value_piece, preferred_element_type=jn...  17.2 us
    dot_general x1, matrix products, attend(): jnp.einsum('qc,kc->qk', queries, key_piece, preferred_element_type=jnp.fl...  14.5 us
    reduce_sum x1, other arithmetic, attend(): denominator = jnp.sum(expo, axis=1)  8.68 us
    dot_general x9, matrix products, local(): jnp.dot(window, w_conv[row_tap, col_tap], preferred_element_type=jnp.floa...  6.07 us
    ppermute x1, waiting for transfers between devices, with_halo(): lax.ppermute(head, axis, [((i + 1) % count, i) for i in range(ends)])  4.35 us
  transfers between devices with their start and end apart: 3, of which 2 were waited for; matrix products, arithmetic and copies ran while one was open for 1% of the time, Pallas kernels for 0%

commit v1 on v0

--- a/solution.py
+++ b/solution.py
@@ -7,6 +7,11 @@
 GROUPS = 32
 W = 128
 epsilon = 1e-06
+
+
+def gather_over(array, axis, along):
+    sent = jnp.stack([array] * lax.axis_size(axis))
+    return jnp.concatenate(lax.all_to_all(sent, axis, 0, 0), axis=along)
 
 
 def copy_for_each(shard, axis):
@@ -99,7 +104,7 @@
         jnp.zeros((count_rows,), jnp.float32),
         jnp.zeros((count_rows, C), jnp.float32),
     )
-    piece = lax.all_gather(normed, "row", axis=0, tiled=True)
+    piece = gather_over(normed, "row", 0)
     key_piece = jnp.dot(piece, w_key, preferred_element_type=jnp.float32).astype(jnp.bfloat16)
     value_piece = jnp.dot(piece, w_value, preferred_element_type=jnp.float32).astype(jnp.bfloat16)
     maxima, denominator, accumulated = attend(start_carry, key_piece, value_piece, queries)

time: 157 us -> 284 us (1.81)
  waiting for transfers between devices: 55.5 us -> 187 us
  between operations: 13.6 us -> 0.26 us
  starting transfers between devices: 4.64 us -> 9.9 us
  local copies, waits for them, and re-layouts: 1.52 us -> 5.56 us
    all_to_all x0 -> x1, waiting for transfers between devices: none -> 183 us  [gather_over(): return jnp.concatenate(lax.all_to_all(sent, axis, 0, 0), axis=along)]
    all_gather x1 -> x0, waiting for transfers between devices: 51.1 us -> none  [local(): piece = lax.all_gather(normed, 'row', axis=0, tiled=True)]
    all_to_all x0 -> x1, starting transfers between devices: none -> 5.26 us  [gather_over(): return jnp.concatenate(lax.all_to_all(sent, axis, 0, 0), axis=along)]
    another operation x0 -> x1, local copies, waits for them, and re-layouts: none -> 4.03 us  [gather_over(): sent = jnp.stack([array] * lax.axis_size(axis))]
  transfers between devices with their start and end apart: 3 -> 3, of which waited for: 2 -> 2; matrix products, arithmetic and copies ran while one was open for 1% -> 0% of each run, Pallas kernels for 0% -> 0%
where the time goes in v1:
time: 284 us
  waiting for transfers between devices  187 us (66%)
  matrix products  38.7 us (14%)
  blocking collectives  29.3 us (10%)
  other arithmetic  12.9 us (5%)
  starting transfers between devices  9.9 us (3%)
  local copies, waits for them, and re-layouts  5.56 us (2%)
    all_to_all x1, waiting for transfers between devices, gather_over(): return jnp.concatenate(lax.all_to_all(sent, axis, 0, 0), axis=along)  183 us
    all_to_all x2, blocking collectives, copy_for_each(): return lax.all_to_all(copies, axis, split_axis=0, concat_axis=0, tiled=True)  29.3 us
    dot_general x1, matrix products, attend(): jnp.dot(expo.astype(jnp.bfloat16), value_piece, preferred_element_type=jn...  17.2 us
    dot_general x1, matrix products, attend(): jnp.einsum('qc,kc->qk', queries, key_piece, preferred_element_type=jnp.fl...  14.5 us
    reduce_sum x1, other arithmetic, attend(): denominator = jnp.sum(expo, axis=1)  8.68 us
    dot_general x9, matrix products, local(): jnp.dot(window, w_conv[row_tap, col_tap], preferred_element_type=jnp.floa...  6.07 us
  transfers between devices with their start and end apart: 3, of which 2 were waited for; matrix products, arithmetic and copies ran while one was open for 0% of the time, Pallas kernels for 0%

profile of v1, /device:TPU:1, one launch (start us, length us, event | category | flops | bytes accessed | tf_op | source)
XLA Modules:
  0.0 283.9 jit_solution(824836749497614837)
XLA Ops:
  0.0 0.0 copy-start
  0.0 1.3 convert_reduce_fusion.1
  1.3 0.1 reduce_sum.74
  1.4 0.1 reduce_sum.80
  1.4 0.1 reduce_sum.75
  1.6 0.1 reduce_sum.96
  1.7 0.1 pad_maximum_fusion.2
  1.8 16.8 %all_to_all.17 = f32[16,1,64]{2,1,0:T(1,128)S(1)} all-to-all(f32[16,1,64]{2,1,0:T(1,128)S(1)} %broadcast_in_dim.6), channel_id=1, replica_groups=mesh['img'=16,'row'=16] {'row'}, dimensions={0} | all-to-all | bytes 8192 | tf_op jit(solution)/shard_map/all_to_all | solution.py:19
  18.6 0.1 slice_multiply_fusion.1
  18.7 0.1 sub.42
  18.7 0.1 sub.43
  18.8 0.1 mul.72
  18.9 0.1 mul.73
  19.0 1.3 fusion.31
  20.2 4.0 %stack.2 = bf16[16,512,512]{2,1,0:T(8,128)(2,1)} broadcast(bf16[512,512]{1,0:T(8,128)(2,1)S(1)} %fusion.31), dimensions={1,2} | broadcast | bytes 8912896 | tf_op jit(solution)/shard_map/stack | solution.py:13
  24.3 5.3 %all-to-all-start.1 = ((bf16[16,512,512]{2,1,0:T(8,128)(2,1)}), bf16[16,512,512]{2,1,0:T(8,128)(2,1)}, u32[]{:S(2)}, u32[]{:S(2)}) async-start(bf16[16,512,512]{2,1,0:T(8,128)(2,1)} %stack.2), calls=%async_computation.1 | async-start | bytes 16777216 | tf_op jit(solution)/shard_map/all_to_all | solution.py:14
  29.5 0.0 copy-done.2
  29.5 0.4 convolution_convert_fusion.2
  30.0 183.0 %all-to-all-done.1 = bf16[16,512,512]{2,1,0:T(8,128)(2,1)} async-done(((bf16[16,512,512]{2,1,0:T(8,128)(2,1)}), bf16[16,512,512]{2,1,0:T(8,128)(2,1)}, u32[]{:S(2)}, u32[]{:S(2)}) %all-to-all-start.1) | async-done | bytes 8388640 | tf_op jit(solution)/shard_map/all_to_all | solution.py:14
  213.0 0.0 copy-done
  213.0 14.5 %multiply_reduce_fusion = (f32[512]{0:T(512)S(1)}, f32[512,8192]{1,0:T(8,128)}) fusion(bf16[512,512]{1,0:T(8,128)(2,1)S(1)} %convolution_convert_fusion.2, bf16[8192,512]{1,0:T(8,128)(2,1)} %bitcast.2, bf16[512,512]{1,0:T(8,128)(2,1)S(1)} %copy-done), kind=kOutput, calls=%fused_computation.1 | convolution fusion | flops 8602517504 | bytes 26216448 | tf_op jit(solution)/shard_map/qc,kc->qk/dot_general | solution.py:73
  227.5 8.7 %fusion = f32[512]{0:T(512)S(1)} fusion(f32[512,8192]{1,0:T(8,128)} %get-tuple-element.24, f32[512]{0:T(512)S(1)} %broadcast_maximum_fusion), kind=kLoop, calls=%fused_computation.2 | loop fusion | flops 12582400 | bytes 16781312 | tf_op jit(solution)/shard_map/reduce_sum | solution.py:77
  236.2 0.0 copy-done.6
  236.2 0.0 copy-start.1
  236.2 0.0 copy-start.7
  236.2 0.0 copy-start.3
  236.2 0.0 copy-start.4
  236.2 17.2 %fusion.15 = bf16[512,512]{1,0:T(8,128)(2,1)S(1)} fusion(bf16[8192,512]{1,0:T(8,128)(2,1)} %bitcast.2, bf16[512,512]{1,0:T(8,128)(2,1)S(1)} %copy-done.6, f32[512,8192]{1,0:T(8,128)} %get-tuple-element.24, f32[512]{0:T(512)S(1)} %broadcast_maximum_fusion, f32[512]{0:T(512)S(1)} %fusion), kind=kOutput, calls=%fused_computation.31 | convolution fusion | flops 8607236096 | bytes 26218496 | tf_op jit(solution)/shard_map/dot_general | solution.py:78
  253.4 0.0 slice-start
  253.4 0.0 copy-done.1
  253.5 0.5 convert_reduce_fusion
  254.0 0.1 reduce_sum.100
  254.0 0.3 reduce_sum.101
  254.3 0.1 reduce_sum.103
  254.4 0.1 reduce_sum.104
  254.5 0.1 pad_maximum_fusion.3
  254.6 12.4 %all_to_all.18 = f32[16,1,64]{2,1,0:T(1,128)S(1)} all-to-all(f32[16,1,64]{2,1,0:T(1,128)S(1)} %broadcast_in_dim.8), channel_id=1, replica_groups=mesh['img'=16,'row'=16] {'row'}, dimensions={0} | all-to-all | bytes 8192 | tf_op jit(solution)/shard_map/all_to_all | solution.py:19
  267.1 0.1 slice_multiply_fusion
  267.1 0.1 sub.49
  267.2 0.1 sub.50
  267.3 0.1 mul.82
  267.4 0.1 mul.83
  267.5 0.0 copy-done.4
  267.5 0.4 fusion.27
  267.9 2.7 collective-permute-start
  270.6 1.9 collective-permute-start.1
  272.5 0.0 collective-permute-done
  272.5 4.3 %collective-permute-done.1 = bf16[1,128,512]{2,1,0:T(8,128)(2,1)S(1)} collective-permute-done((bf16[1,128,512]{2,1,0:T(8,128)(2,1)S(1)}, bf16[1,128,512]{2,1,0:T(8,128)(2,1)S(1)}, u32[]{:S(2)}, u32[]{:S(2)}) %collective-permute-start.1) | collective-permute-done | bytes 131104 | tf_op jit(solution)/shard_map/ppermute | solution.py:45
  276.9 0.2 fusion.36
  277.1 0.0 slice-start.1
  277.1 0.4 fusion.58
  277.5 1.7 fusion.46
  279.2 0.1 pad_maximum_fusion
  279.3 0.1 slice-done.1
  279.4 0.4 convolution_add_fusion.6
  279.9 0.0 copy-start.5
  279.9 0.4 convolution_add_fusion.5
  280.4 0.4 convolution_add_fusion.4
  280.8 0.4 convolution_add_fusion.3
  281.3 0.4 fusion.37
  281.7 0.4 convolution_add_fusion.2
  282.1 0.4 convolution_add_fusion.1
  282.6 0.0 copy-done.5
  282.6 1.3 fusion.10
  (12 shorter events, 0.1 us)
Async XLA Ops:
  0.0 213.0 %copy-start = (bf16[512,512]{1,0:T(8,128)(2,1)S(1)}, bf16[512,512]{1,0:T(8,128)(2,1)}, u32[]{:S(2)}) copy-start(bf16[512,512]{1,0:T(8,128)(2,1)} %param.15) | copy-start | bytes 1572868
  24.3 5.3 %copy-start.2 = (bf16[512,512]{1,0:T(8,128)(2,1)S(1)}, bf16[512,512]{1,0:T(8,128)(2,1)}, u32[]{:S(2)}) copy-start(bf16[512,512]{1,0:T(8,128)(2,1)} %param.14) | copy-start | bytes 1572868
  24.3 188.7 %all-to-all-start.1 = ((bf16[16,512,512]{2,1,0:T(8,128)(2,1)}), bf16[16,512,512]{2,1,0:T(8,128)(2,1)}, u32[]{:S(2)}, u32[]{:S(2)}) async-start(bf16[16,512,512]{2,1,0:T(8,128)(2,1)} %stack.2), calls=%async_computation.1 | async-start | bytes 16777216 | tf_op jit(solution)/shard_map/all_to_all | solution.py:14
  227.5 8.7 %copy-start.6 = (bf16[512,512]{1,0:T(8,128)(2,1)S(1)}, bf16[512,512]{1,0:T(8,128)(2,1)}, u32[]{:S(2)}) copy-start(bf16[512,512]{1,0:T(8,128)(2,1)} %param.16) | copy-start | bytes 1572868
  236.2 17.2 %copy-start.1 = (bf16[4,128,512]{2,1,0:T(8,128)(2,1)S(1)}, bf16[4,128,512]{2,1,0:T(8,128)(2,1)}, u32[]{:S(2)}) copy-start(bf16[4,128,512]{2,1,0:T(8,128)(2,1)} %param.11) | copy-start | bytes 1572868
  236.2 17.2 %copy-start.7 = (bf16[512,512]{1,0:T(8,128)(2,1)S(1)}, bf16[512,512]{1,0:T(8,128)(2,1)}, u32[]{:S(2)}) copy-start(bf16[512,512]{1,0:T(8,128)(2,1)} %param.17) | copy-start | bytes 1572868
  236.2 31.2 %copy-start.3 = (f32[512]{0:T(512)S(1)}, f32[512]{0:T(512)}, u32[]{:S(2)}) copy-start(f32[512]{0:T(512)} %param.19) | copy-start | bytes 6148
  236.2 31.2 %copy-start.4 = (f32[512]{0:T(512)S(1)}, f32[512]{0:T(512)}, u32[]{:S(2)}) copy-start(f32[512]{0:T(512)} %param.18) | copy-start | bytes 6148
  253.4 25.9 %slice-start = ((s8[4718592]{0:T(1024)(128)(4,1)}), s8[524288]{0:T(1024)(128)(4,1)S(1)}, s32[]{:S(2)}) async-start(s8[4718592]{0:T(1024)(128)(4,1)} %bitcast.75), calls=%async_computation.3 | async-start | bytes 1048576
  267.9 4.7 %collective-permute-start = (bf16[1,128,512]{2,1,0:T(8,128)(2,1)S(1)}, bf16[1,128,512]{2,1,0:T(8,128)(2,1)S(1)}, u32[]{:S(2)}, u32[]{:S(2)}) collective-permute-start(bf16[1,128,512]{2,1,0:T(8,128)(2,1)S(1)} %get-tuple-element.17), channel_id=1, source_target_pairs={{0,1},{1,2},{2,3},{3,4},{4,5},{5,6},{6,7},{7,8},{8,9},{9,10},{10,1... | collective-permute-start | bytes 393224 | tf_op jit(solution)/shard_map/ppermute | solution.py:43
  270.6 6.3 %collective-permute-start.1 = (bf16[1,128,512]{2,1,0:T(8,128)(2,1)S(1)}, bf16[1,128,512]{2,1,0:T(8,128)(2,1)S(1)}, u32[]{:S(2)}, u32[]{:S(2)}) collective-permute-start(bf16[1,128,512]{2,1,0:T(8,128)(2,1)S(1)} %get-tuple-element.18), channel_id=1, source_target_pairs={{1,0},{2,1},{3,2},{4,3},{5,4},{6,5},{7,6},{8,7},{9,8},{10,9},{11,1... | collective-permute-start | bytes 393224 | tf_op jit(solution)/shard_map/ppermute | solution.py:45
  277.1 2.3 slice-start.1
  279.9 2.7 copy-start.5
